TPU v7x, 32 devices: a whole 2x2x4 slice. The times are simulated.
32 devices in a mesh: sfc: 16 (over z, y, x), grp: 2 (over core).
Axes of the slice: x: 2, y: 2, z: 4, core: 2. Of those that a mesh axis runs over, the one named last changes fastest.
Arguments:
- right_side: float32 [5, 5, 5, 4096], P(None, None, None, ('sfc', 'grp')), may hold values from -8 to 8
- cell_level: int32 [4096], P(('sfc', 'grp')), may hold values from 0 to 3
- own_slot: int32 [12288], P(('sfc', 'grp')), may hold values from 0 to 767
- near_slot: int32 [12288], P(('sfc', 'grp')), may hold values from 0 to 1151, as said below
- face_kind: int32 [12288], P(('sfc', 'grp')), may hold values from 0 to 5
- orientation: int32 [12288], P(('sfc', 'grp')), may hold values from 0 to 7
- penalty: float32 [12288], P(('sfc', 'grp')), may hold values from 2 to 32
- send_slots: int32 [12288], P(('sfc', 'grp')), may hold values from 0 to 767
- subface_maps: float32 [4, 25, 25], replicated, may hold values from -1.25 to 1.25
Outputs:
- solution: float32 [5, 5, 5, 4096], P(None, None, None, ('sfc', 'grp'))
- residual: float32 [5, 5, 5, 4096], P(None, None, None, ('sfc', 'grp'))
Inputs may be any that keep to these rules, and one draw needn't show every extreme that they name: `own_slot`: a face slot f * 128 + c of the same device. `near_slot`: 768 + k * 96 + i for position i of the received block k; since a device has exactly 384 entries, its near slots are a permutation of its 384 received positions. `face_kind`: 0 boundary face, 1 conforming face, 2 + s the fine side of a hanging face with subface s. `send_slots`: a device's entries k * 96 to k * 96 + 95 are face slots of its own cells sent to the device at offset (+1, -1, +2, -2)[k].
All inputs are finite; a program needn't handle non-finite values.
Results may differ from a plain program's by a relative error of at most 0.00021.
Values sent between devices are 32-bit elements; how exact they have to be, the bound alone decides.
A program may use at most 64 MiB of HBM per device.

v0:
```python
import jax
import jax.numpy as jnp
import numpy as np
from jax import lax
from jax.sharding import PartitionSpec as P

NODES = 5
ITERS = 3


mass_shift = 1.0
highest = lax.Precision.HIGHEST


def partner_2(block, axis, distance):
    count = lax.axis_size(axis)
    route = []
    for low in range(count):
        high = low | 1 << distance
        if high != low and high < count:
            route += [(low, high), (high, low)]
    return lax.ppermute(block, axis, route)


def shifted(block, axis, distance):
    devices = range(lax.axis_size(axis))
    route = [(i - distance, i) for i in devices if i - distance in devices]
    return lax.ppermute(block, axis, route)


def node_tables():
    points = np.array([-1.0, -np.sqrt(3.0 / 7.0), 0.0, np.sqrt(3.0 / 7.0), 1.0])
    weights = np.array([0.1, 49.0 / 90.0, 32.0 / 45.0, 49.0 / 90.0, 0.1])
    identity = np.eye(5)
    spacing = points[:, None] - points[None, :] + identity
    barycentric = 1.0 / np.prod(spacing, axis=1)
    offdiag = barycentric[None, :] / barycentric[:, None] / spacing
    diagonal = np.sum(1.0 / spacing, axis=1) - 1.0
    derivs = np.where(identity > 0.5, diagonal[:, None], offdiag)
    stiffness = derivs.T @ (weights[:, None] * derivs)
    return (jnp.asarray(stiffness, jnp.float32), jnp.asarray(weights, jnp.float32))


def volume_term(field, scale, tables):
    stiffness, weights = tables
    first = weights[:, None, None, None]
    second = weights[None, :, None, None]
    third = weights[None, None, :, None]
    along_first = jnp.einsum("ia,abcz->ibcz", stiffness, field, precision=highest)
    along_second = jnp.einsum("jb,abcz->ajcz", stiffness, field, precision=highest)
    along_third = jnp.einsum("kc,abcz->abkz", stiffness, field, precision=highest)
    grads = (
        along_first * second * third + along_second * first * third + along_third * first * second
    )
    return scale * grads + mass_shift * scale * scale * scale * first * second * third * field


def face_traces(field):
    last = NODES - 1
    return jnp.stack(
        [field[0], field[last], field[:, 0], field[:, last], field[:, :, 0], field[:, :, last]],
        axis=-2,
    )


def lift_faces(faces):
    last = NODES - 1
    rest = faces.shape[2:-2] + faces.shape[-1:]
    volume = jnp.zeros((NODES, NODES, NODES) + rest, faces.dtype)
    volume = volume.at[0].add(faces[..., 0, :])
    volume = volume.at[last].add(faces[..., 1, :])
    volume = volume.at[:, 0].add(faces[..., 2, :])
    volume = volume.at[:, last].add(faces[..., 3, :])
    volume = volume.at[:, :, 0].add(faces[..., 4, :])
    volume = volume.at[:, :, last].add(faces[..., 5, :])
    return volume


def orient_forward(values, codes):
    values = jnp.where(codes & 1 == 1, values[::-1], values)
    values = jnp.where(codes & 2 == 2, values[:, ::-1], values)
    return jnp.where(codes & 4 == 4, jnp.swapaxes(values, 0, 1), values)


def orient_back(values, codes):
    values = jnp.where(codes & 4 == 4, jnp.swapaxes(values, 0, 1), values)
    values = jnp.where(codes & 2 == 2, values[:, ::-1], values)
    return jnp.where(codes & 1 == 1, values[::-1], values)


def map_traces(values, kinds, maps, transpose_maps):
    width = NODES * NODES
    flat = values.reshape(width, -1)
    stacked = jnp.swapaxes(maps, 1, 2) if transpose_maps else maps
    moved = jnp.dot(stacked.reshape(4 * width, width), flat, precision=highest).reshape(
        4, width, -1
    )
    selector = kinds[None, :] == jnp.arange(4, dtype=jnp.int32)[:, None] + 2
    result = jnp.where(kinds == 1, flat, 0.0) + jnp.sum(
        jnp.where(selector[:, None, :], moved, 0.0), axis=0
    )
    return result.reshape(values.shape)


def face_terms(own_values, near_values, kinds, orients, penalty, maps, weights):
    face_mass = weights[:, None, None] * weights[None, :, None]
    mapped = map_traces(orient_forward(near_values, orients), kinds, maps, False)
    jump = own_values - mapped
    own_term = penalty * face_mass * jump
    near_term = -orient_back(map_traces(own_term, kinds, maps, True), orients)
    return (own_term, near_term)


def route_blocks(blocks):
    core = lax.axis_index("grp")
    partner = partner_2(jnp.stack([blocks[0], blocks[1]]), "grp", 0)
    upward = shifted(jnp.stack([blocks[2], partner[0]]), "sfc", 1)
    downward = shifted(jnp.stack([blocks[3], partner[1]]), "sfc", -1)
    plus_one = jnp.where(core == 1, partner[0], upward[1])
    minus_one = jnp.where(core == 0, partner[1], downward[1])
    return (plus_one, minus_one, upward[0], downward[0])


def apply_operator(
    field, scale, own_slot, near_slot, kinds, orients, penalty, send_slots, maps, tables
):
    count = field.shape[-1]
    slots = 6 * count
    width = NODES * NODES
    ghost = send_slots.shape[0] // 4
    traces = face_traces(field).reshape(width, slots)
    sent = jnp.take(traces, send_slots, axis=1)
    arrived = route_blocks(
        tuple((sent[:, position * ghost : (position + 1) * ghost] for position in range(4)))
    )
    volume = volume_term(field, scale, tables)
    pool = jnp.concatenate((traces,) + arrived, axis=1)
    own_values = jnp.take(pool, own_slot, axis=1).reshape(NODES, NODES, -1)
    near_values = jnp.take(pool, near_slot, axis=1).reshape(NODES, NODES, -1)
    own_term, near_term = face_terms(
        own_values, near_values, kinds, orients, penalty, maps, tables[1]
    )
    gathered = jnp.zeros_like(pool).at[:, own_slot].add(own_term.reshape(width, -1))
    gathered = gathered.at[:, near_slot].add(near_term.reshape(width, -1))
    returned = tuple(
        (
            gathered[:, slots + position * ghost : slots + (position + 1) * ghost]
            for position in range(4)
        )
    )
    came_back = route_blocks((returned[1], returned[0], returned[3], returned[2]))
    back = jnp.concatenate((came_back[1], came_back[0], came_back[3], came_back[2]), axis=1)
    local = gathered[:, :slots].at[:, send_slots].add(back)
    faces = local.reshape(NODES, NODES, 6, count)
    return volume + lift_faces(faces)


def body(
    right_side,
    cell_level,
    own_slot,
    near_slot,
    face_kind,
    orientation,
    penalty,
    send_slots,
    subface_maps,
):
    tables = node_tables()
    scale = jnp.exp2(-cell_level.astype(jnp.float32))
    count = right_side.shape[-1]
    scaled_penalty = penalty * jnp.take(scale, own_slot % count)
    solution = jnp.zeros_like(right_side)
    residual = right_side
    direction = right_side
    for iteration in range(ITERS):
        image = apply_operator(
            direction,
            scale,
            own_slot,
            near_slot,
            face_kind,
            orientation,
            scaled_penalty,
            send_slots,
            subface_maps,
            tables,
        )
        totals = lax.psum(
            (
                jnp.sum(residual * residual),
                jnp.sum(direction * image),
                jnp.sum(residual * image),
                jnp.sum(image * image),
            ),
            ("sfc", "grp"),
        )
        norm_now = totals[0]
        step_size = norm_now / totals[1]
        solution = solution + step_size * direction
        residual = residual - step_size * image
        if iteration + 1 < ITERS:
            norm_next = norm_now - 2.0 * step_size * totals[2] + step_size * step_size * totals[3]
            direction = residual + norm_next / norm_now * direction
    return (solution, residual)


def solution(mesh):
    return jax.shard_map(
        body,
        mesh=mesh,
        in_specs=(
            P(None, None, None, ("sfc", "grp")),
            P(("sfc", "grp")),
            P(("sfc", "grp")),
            P(("sfc", "grp")),
            P(("sfc", "grp")),
            P(("sfc", "grp")),
            P(("sfc", "grp")),
            P(("sfc", "grp")),
            P(),
        ),
        out_specs=(P(None, None, None, ("sfc", "grp")), P(None, None, None, ("sfc", "grp"))),
        check_vma=False,
    )
```

profile of v0, /device:TPU:0, one launch (start us, length us, event | category | flops | bytes accessed | tf_op | source)
XLA Modules:
  0.0 261.0 jit_solution(8672234556386529940)
XLA Ops:
  8.5 2.7 %gather_fusion = f32[384]{0:T(512)S(1)} fusion(f32[128]{0:T(128)S(1)} %get-tuple-element.341, s32[1024]{0:T(1024)S(1)} %get-tuple-element.348), kind=kCustom, calls=%fused_computation.9 | custom fusion | bytes 4608 | tf_op jit(solution)/shard_map/jit(_take)/gather | solution.py:172
  11.6 1.3 collective-permute-start.2
  13.0 5.5 %collective-permute-start.1 = (f32[2,25,96]{2,0,1:T(2,128)S(1)}, f32[2,25,96]{2,0,1:T(2,128)S(1)}, u32[]{:S(2)}, u32[]{:S(2)}) collective-permute-start(f32[2,25,96]{2,0,1:T(2,128)S(1)} %pad_maximum_fusion.1), channel_id=1, source_target_pairs={{0,2},{2,4},{4,6},{6,8},{8,10},{10,12},{12,14},{14,16},{16,18},{18... | collective-permute-start | bytes 57608 | tf_op jit(solution)/shard_map/ppermute | solution.py:28
  18.8 1.2 collective-permute-done.1
  20.5 1.1 gather_fusion.2
  21.9 1.1 gather_fusion.3
  24.1 2.0 scatter_custom_fusion
  27.0 2.8 %scatter_fusion = f32[25,1152]{0,1:T(8,128)S(1)} fusion(f32[25,1152]{0,1:T(8,128)S(1)} %scatter_custom_fusion, s32[384]{0:T(512)S(1)} %get-tuple-element.343, f32[384,25]{1,0:T(8,128)S(1)} %copy.195), kind=kCustom, calls=%fused_computation.11 | custom fusion | flops 9600 | bytes 116736 | tf_op jit(solution)/shard_map/scatter-add | solution.py:144
  31.4 1.3 collective-permute-start.4
  32.7 5.4 %collective-permute-start.5 = (f32[2,25,96]{2,0,1:T(2,128)S(1)}, f32[2,25,96]{2,0,1:T(2,128)S(1)}, u32[]{:S(2)}, u32[]{:S(2)}) collective-permute-start(f32[2,25,96]{2,0,1:T(2,128)S(1)} %pad_maximum_fusion.5), channel_id=1, source_target_pairs={{0,2},{2,4},{4,6},{6,8},{8,10},{10,12},{12,14},{14,16},{16,18},{18... | collective-permute-start | bytes 57608 | tf_op jit(solution)/shard_map/ppermute | solution.py:28
  40.0 2.8 %scatter_fusion.1 = f32[25,768]{0,1:T(8,128)S(1)} fusion(f32[25,768]{0,1:T(8,128)S(1)} %slice.925, s32[384]{0:T(512)S(1)} %get-tuple-element.344, f32[384,25]{1,0:T(8,128)S(1)} %copy.200), kind=kCustom, calls=%fused_computation.12 | custom fusion | flops 9600 | bytes 116736 | tf_op jit(solution)/shard_map/scatter-add | solution.py:153
  44.2 46.1 %all-reduce.5 = (f32[]{:T(128)}, f32[]{:T(128)}, f32[]{:T(128)}) all-reduce(f32[]{:T(128)} %multiply_reduce_fusion.8, f32[]{:T(128)} %get-tuple-element.231, f32[]{:T(128)} %get-tuple-element.230), channel_id=1, replica_groups=mesh['sfc'=16,'grp'=2] {'sfc','grp'}, use_global_device_ids=true, to_apply=%region_1.2 | all-reduce | flops 3 | bytes 24 | tf_op jit(solution)/shard_map/psum | solution.py:189
  97.5 1.3 collective-permute-start.8
  98.8 4.8 %collective-permute-start.7 = (f32[2,25,96]{2,0,1:T(2,128)S(1)}, f32[2,25,96]{2,0,1:T(2,128)S(1)}, u32[]{:S(2)}, u32[]{:S(2)}) collective-permute-start(f32[2,25,96]{2,0,1:T(2,128)S(1)} %pad_maximum_fusion.7), channel_id=1, source_target_pairs={{0,2},{2,4},{4,6},{6,8},{8,10},{10,12},{12,14},{14,16},{16,18},{18... | collective-permute-start | bytes 57608 | tf_op jit(solution)/shard_map/ppermute | solution.py:28
  103.8 1.4 collective-permute-done.7
  109.7 2.0 scatter_custom_fusion.3
  112.1 2.8 %scatter_fusion.2 = f32[25,1152]{0,1:T(8,128)S(1)} fusion(f32[25,1152]{0,1:T(8,128)S(1)} %scatter_custom_fusion.3, s32[384]{0:T(512)S(1)} %get-tuple-element.343, f32[384,25]{1,0:T(8,128)S(1)} %copy.237), kind=kCustom, calls=%fused_computation.14 | custom fusion | flops 9600 | bytes 116736 | tf_op jit(solution)/shard_map/scatter-add | solution.py:144
  116.5 1.3 collective-permute-start.10
  117.9 5.4 %collective-permute-start.11 = (f32[2,25,96]{2,0,1:T(2,128)S(1)}, f32[2,25,96]{2,0,1:T(2,128)S(1)}, u32[]{:S(2)}, u32[]{:S(2)}) collective-permute-start(f32[2,25,96]{2,0,1:T(2,128)S(1)} %pad_maximum_fusion.11), channel_id=1, source_target_pairs={{0,2},{2,4},{4,6},{6,8},{8,10},{10,12},{12,14},{14,16},{16,18},{18... | collective-permute-start | bytes 57608 | tf_op jit(solution)/shard_map/ppermute | solution.py:28
  123.4 1.5 collective-permute-done.11
  125.3 2.8 %scatter_fusion.3 = f32[25,768]{0,1:T(8,128)S(1)} fusion(f32[25,768]{0,1:T(8,128)S(1)} %slice.962, s32[384]{0:T(512)S(1)} %get-tuple-element.344, f32[384,25]{1,0:T(8,128)S(1)} %copy.242), kind=kCustom, calls=%fused_computation.15 | custom fusion | flops 9600 | bytes 116736 | tf_op jit(solution)/shard_map/scatter-add | solution.py:153
  129.2 44.8 %all-reduce.4 = (f32[]{:T(128)}, f32[]{:T(128)}, f32[]{:T(128)}, f32[]{:T(128)}) all-reduce(f32[]{:T(128)} %get-tuple-element.228, f32[]{:T(128)} %get-tuple-element.229, f32[]{:T(128)} %get-tuple-element.227, f32[]{:T(128)} %get-tuple-element.226), channel_id=1, replica_groups=mesh['sfc'=16,'grp'=2] {'sfc','grp'}, use_global_device_ids=true, to_apply=%region_10.13 | all-reduce | flops 4 | bytes 32 | tf_op jit(solution)/shard_map/psum | solution.py:189
  182.2 1.3 collective-permute-start.14
  183.6 4.8 %collective-permute-start.13 = (f32[2,25,96]{2,0,1:T(2,128)S(1)}, f32[2,25,96]{2,0,1:T(2,128)S(1)}, u32[]{:S(2)}, u32[]{:S(2)}) collective-permute-start(f32[2,25,96]{2,0,1:T(2,128)S(1)} %pad_maximum_fusion.13), channel_id=1, source_target_pairs={{0,2},{2,4},{4,6},{6,8},{8,10},{10,12},{12,14},{14,16},{16,18},{18... | collective-permute-start | bytes 57608 | tf_op jit(solution)/shard_map/ppermute | solution.py:28
  188.5 1.4 collective-permute-done.13
  194.4 2.0 scatter_custom_fusion.6
  196.8 2.8 %scatter_fusion.4 = f32[25,1152]{0,1:T(8,128)S(1)} fusion(f32[25,1152]{0,1:T(8,128)S(1)} %scatter_custom_fusion.6, s32[384]{0:T(512)S(1)} %get-tuple-element.343, f32[384,25]{1,0:T(8,128)S(1)} %copy.273), kind=kCustom, calls=%fused_computation.17 | custom fusion | flops 9600 | bytes 116736 | tf_op jit(solution)/shard_map/scatter-add | solution.py:144
  201.2 1.3 collective-permute-start.16
  202.6 5.4 %collective-permute-start.17 = (f32[2,25,96]{2,0,1:T(2,128)S(1)}, f32[2,25,96]{2,0,1:T(2,128)S(1)}, u32[]{:S(2)}, u32[]{:S(2)}) collective-permute-start(f32[2,25,96]{2,0,1:T(2,128)S(1)} %pad_maximum_fusion.17), channel_id=1, source_target_pairs={{0,2},{2,4},{4,6},{6,8},{8,10},{10,12},{12,14},{14,16},{16,18},{18... | collective-permute-start | bytes 57608 | tf_op jit(solution)/shard_map/ppermute | solution.py:28
  208.2 1.3 collective-permute-done.17
  209.9 2.8 %scatter_fusion.5 = f32[25,768]{0,1:T(8,128)S(1)} fusion(f32[25,768]{0,1:T(8,128)S(1)} %slice.999, s32[384]{0:T(512)S(1)} %get-tuple-element.344, f32[384,25]{1,0:T(8,128)S(1)} %copy.278), kind=kCustom, calls=%fused_computation.18 | custom fusion | flops 9600 | bytes 116736 | tf_op jit(solution)/shard_map/scatter-add | solution.py:153
  213.7 44.6 %all-reduce.3 = (f32[]{:T(128)}, f32[]{:T(128)}) all-reduce(f32[]{:T(128)} %get-tuple-element.241, f32[]{:T(128)} %multiply_reduce_fusion), channel_id=1, replica_groups=mesh['sfc'=16,'grp'=2] {'sfc','grp'}, use_global_device_ids=true, to_apply=%region_21.24 | all-reduce | flops 2 | bytes 16 | tf_op jit(solution)/shard_map/psum | solution.py:189
  (337 shorter events, 39.8 us)
Async XLA Ops:
  0.6 1.0 copy-start
  1.9 0.7 copy-start.6
  2.6 0.7 copy-start.7
  4.7 0.7 copy-start.4
  4.8 6.8 %collective-permute-start = (f32[2,25,96]{2,0,1:T(2,128)S(1)}, f32[2,25,96]{2,0,1:T(2,128)S(1)}, u32[]{:S(2)}, u32[]{:S(2)}) collective-permute-start(f32[2,25,96]{2,0,1:T(2,128)S(1)} %pad_maximum_fusion), channel_id=1, source_target_pairs={{0,1},{1,0},{2,3},{3,2},{4,5},{5,4},{6,7},{7,6},{8,9},{9,8},{10,11... | collective-permute-start | bytes 57608 | tf_op jit(solution)/shard_map/ppermute | solution.py:22
  5.5 0.7 copy-start.2
  6.1 0.7 copy-start.10
  6.9 0.7 copy-start.1
  7.8 0.7 copy-start.5
  7.8 0.7 copy-start.8
  8.5 2.7 %copy-start.9 = (f32[384]{0:T(512)S(1)}, f32[384]{0:T(512)}, u32[]{:S(2)}) copy-start(f32[384]{0:T(512)} %param.57) | copy-start | bytes 4612
  11.6 6.9 %copy-start.3 = (f32[4,25,25]{2,0,1:T(4,128)S(1)}, f32[4,25,25]{2,0,1:T(4,128)}, u32[]{:S(2)}) copy-start(f32[4,25,25]{2,0,1:T(4,128)} %param.59) | copy-start | bytes 30004
  11.6 7.2 %collective-permute-start.2 = (f32[2,25,96]{2,0,1:T(2,128)S(1)}, f32[2,25,96]{2,0,1:T(2,128)S(1)}, u32[]{:S(2)}, u32[]{:S(2)}) collective-permute-start(f32[2,25,96]{2,0,1:T(2,128)S(1)} %pad_maximum_fusion.2), channel_id=1, source_target_pairs={{2,0},{4,2},{6,4},{8,6},{10,8},{12,10},{14,12},{16,14},{18,16},{20... | collective-permute-start | bytes 57608 | tf_op jit(solution)/shard_map/ppermute | solution.py:28
  13.0 7.0 %collective-permute-start.1 = (f32[2,25,96]{2,0,1:T(2,128)S(1)}, f32[2,25,96]{2,0,1:T(2,128)S(1)}, u32[]{:S(2)}, u32[]{:S(2)}) collective-permute-start(f32[2,25,96]{2,0,1:T(2,128)S(1)} %pad_maximum_fusion.1), channel_id=1, source_target_pairs={{0,2},{2,4},{4,6},{6,8},{8,10},{10,12},{12,14},{14,16},{16,18},{18... | collective-permute-start | bytes 57608 | tf_op jit(solution)/shard_map/ppermute | solution.py:28
  30.0 1.3 collective-permute-start.3
  31.4 7.4 %collective-permute-start.4 = (f32[2,25,96]{2,0,1:T(2,128)S(1)}, f32[2,25,96]{2,0,1:T(2,128)S(1)}, u32[]{:S(2)}, u32[]{:S(2)}) collective-permute-start(f32[2,25,96]{2,0,1:T(2,128)S(1)} %pad_maximum_fusion.4), channel_id=1, source_target_pairs={{2,0},{4,2},{6,4},{8,6},{10,8},{12,10},{14,12},{16,14},{18,16},{20... | collective-permute-start | bytes 57608 | tf_op jit(solution)/shard_map/ppermute | solution.py:28
  32.7 6.9 %collective-permute-start.5 = (f32[2,25,96]{2,0,1:T(2,128)S(1)}, f32[2,25,96]{2,0,1:T(2,128)S(1)}, u32[]{:S(2)}, u32[]{:S(2)}) collective-permute-start(f32[2,25,96]{2,0,1:T(2,128)S(1)} %pad_maximum_fusion.5), channel_id=1, source_target_pairs={{0,2},{2,4},{4,6},{6,8},{8,10},{10,12},{12,14},{14,16},{16,18},{18... | collective-permute-start | bytes 57608 | tf_op jit(solution)/shard_map/ppermute | solution.py:28
  96.2 1.3 collective-permute-start.6
  97.5 6.3 %collective-permute-start.8 = (f32[2,25,96]{2,0,1:T(2,128)S(1)}, f32[2,25,96]{2,0,1:T(2,128)S(1)}, u32[]{:S(2)}, u32[]{:S(2)}) collective-permute-start(f32[2,25,96]{2,0,1:T(2,128)S(1)} %pad_maximum_fusion.8), channel_id=1, source_target_pairs={{2,0},{4,2},{6,4},{8,6},{10,8},{12,10},{14,12},{16,14},{18,16},{20... | collective-permute-start | bytes 57608 | tf_op jit(solution)/shard_map/ppermute | solution.py:28
  98.8 6.3 %collective-permute-start.7 = (f32[2,25,96]{2,0,1:T(2,128)S(1)}, f32[2,25,96]{2,0,1:T(2,128)S(1)}, u32[]{:S(2)}, u32[]{:S(2)}) collective-permute-start(f32[2,25,96]{2,0,1:T(2,128)S(1)} %pad_maximum_fusion.7), channel_id=1, source_target_pairs={{0,2},{2,4},{4,6},{6,8},{8,10},{10,12},{12,14},{14,16},{16,18},{18... | collective-permute-start | bytes 57608 | tf_op jit(solution)/shard_map/ppermute | solution.py:28
  115.2 1.3 collective-permute-start.9
  116.5 6.9 %collective-permute-start.10 = (f32[2,25,96]{2,0,1:T(2,128)S(1)}, f32[2,25,96]{2,0,1:T(2,128)S(1)}, u32[]{:S(2)}, u32[]{:S(2)}) collective-permute-start(f32[2,25,96]{2,0,1:T(2,128)S(1)} %pad_maximum_fusion.10), channel_id=1, source_target_pairs={{2,0},{4,2},{6,4},{8,6},{10,8},{12,10},{14,12},{16,14},{18,16},{20... | collective-permute-start | bytes 57608 | tf_op jit(solution)/shard_map/ppermute | solution.py:28
  117.9 7.1 %collective-permute-start.11 = (f32[2,25,96]{2,0,1:T(2,128)S(1)}, f32[2,25,96]{2,0,1:T(2,128)S(1)}, u32[]{:S(2)}, u32[]{:S(2)}) collective-permute-start(f32[2,25,96]{2,0,1:T(2,128)S(1)} %pad_maximum_fusion.11), channel_id=1, source_target_pairs={{0,2},{2,4},{4,6},{6,8},{8,10},{10,12},{12,14},{14,16},{16,18},{18... | collective-permute-start | bytes 57608 | tf_op jit(solution)/shard_map/ppermute | solution.py:28
  180.9 1.3 collective-permute-start.12
  182.2 6.2 %collective-permute-start.14 = (f32[2,25,96]{2,0,1:T(2,128)S(1)}, f32[2,25,96]{2,0,1:T(2,128)S(1)}, u32[]{:S(2)}, u32[]{:S(2)}) collective-permute-start(f32[2,25,96]{2,0,1:T(2,128)S(1)} %pad_maximum_fusion.14), channel_id=1, source_target_pairs={{2,0},{4,2},{6,4},{8,6},{10,8},{12,10},{14,12},{16,14},{18,16},{20... | collective-permute-start | bytes 57608 | tf_op jit(solution)/shard_map/ppermute | solution.py:28
  183.6 6.3 %collective-permute-start.13 = (f32[2,25,96]{2,0,1:T(2,128)S(1)}, f32[2,25,96]{2,0,1:T(2,128)S(1)}, u32[]{:S(2)}, u32[]{:S(2)}) collective-permute-start(f32[2,25,96]{2,0,1:T(2,128)S(1)} %pad_maximum_fusion.13), channel_id=1, source_target_pairs={{0,2},{2,4},{4,6},{6,8},{8,10},{10,12},{12,14},{14,16},{16,18},{18... | collective-permute-start | bytes 57608 | tf_op jit(solution)/shard_map/ppermute | solution.py:28
  199.9 1.3 collective-permute-start.15
  201.2 7.0 %collective-permute-start.16 = (f32[2,25,96]{2,0,1:T(2,128)S(1)}, f32[2,25,96]{2,0,1:T(2,128)S(1)}, u32[]{:S(2)}, u32[]{:S(2)}) collective-permute-start(f32[2,25,96]{2,0,1:T(2,128)S(1)} %pad_maximum_fusion.16), channel_id=1, source_target_pairs={{2,0},{4,2},{6,4},{8,6},{10,8},{12,10},{14,12},{16,14},{18,16},{20... | collective-permute-start | bytes 57608 | tf_op jit(solution)/shard_map/ppermute | solution.py:28
  202.6 7.0 %collective-permute-start.17 = (f32[2,25,96]{2,0,1:T(2,128)S(1)}, f32[2,25,96]{2,0,1:T(2,128)S(1)}, u32[]{:S(2)}, u32[]{:S(2)}) collective-permute-start(f32[2,25,96]{2,0,1:T(2,128)S(1)} %pad_maximum_fusion.17), channel_id=1, source_target_pairs={{0,2},{2,4},{4,6},{6,8},{8,10},{10,12},{12,14},{14,16},{16,18},{18... | collective-permute-start | bytes 57608 | tf_op jit(solution)/shard_map/ppermute | solution.py:28
where the time goes:
time: 262 us; the launch traced here: 261 us
  blocking collectives  136 us (52%)
  starting transfers between devices  40.1 us (15%)
  other arithmetic  29.6 us (11%)
  local copies, waits for them, and re-layouts  27.2 us (10%)
  between operations  11.9 us (5%)
  waiting for transfers between devices  11.6 us (4%)
  matrix products  5.04 us (2%)
    psum x3, blocking collectives, body(): lax.psum((jnp.sum(residual * residual), jnp.sum(direction * image), jnp.s...  136 us
    ppermute x12, starting transfers between devices, shifted(): return lax.ppermute(block, axis, route)  39.2 us
    scatter-add x3, other arithmetic, apply_operator(): gathered = gathered.at[:, near_slot].add(near_term.reshape(width, -1))  8.54 us
    scatter-add x3, other arithmetic, apply_operator(): local = gathered[:, :slots].at[:, send_slots].add(back)  8.33 us
    ppermute x12, waiting for transfers between devices, shifted(): return lax.ppermute(block, axis, route)  7.65 us
    unnamed x67, local copies, waits for them, and re-layouts  6.44 us
    scatter-add x3, other arithmetic, apply_operator(): jnp.zeros_like(pool).at[:, own_slot].add(own_term.reshape(width, -1))  5.95 us
  transfers between devices with their start and end apart: 18, of which 11 were waited for; matrix products, arithmetic and copies ran while one was open for 3% of the time, Pallas kernels for 0%

commit v1 on v0

v1 whole, which is shorter than its diff:
```python
import functools

import jax
import jax.numpy as jnp
import numpy as np
from jax import lax
from jax.experimental import pallas as pl
from jax.experimental.pallas import tpu as pltpu
from jax.sharding import PartitionSpec as P

NODES = 5
WIDTH = NODES * NODES
ROWS = 32
CUBE = 128
ITERS = 3
OFFSETS = (1, -1, 2, -2)
MASS = 1.0
MESH = pl.DeviceIdType.MESH
F32 = jnp.float32
BF16 = jnp.bfloat16


def node_tables():
    points = np.array([-1.0, -np.sqrt(3.0 / 7.0), 0.0, np.sqrt(3.0 / 7.0), 1.0])
    weights = np.array([0.1, 49.0 / 90.0, 32.0 / 45.0, 49.0 / 90.0, 0.1])
    identity = np.eye(5)
    spacing = points[:, None] - points[None, :] + identity
    barycentric = 1.0 / np.prod(spacing, axis=1)
    offdiag = barycentric[None, :] / barycentric[:, None] / spacing
    diagonal = np.sum(1.0 / spacing, axis=1) - 1.0
    derivs = np.where(identity > 0.5, diagonal[:, None], offdiag)
    return derivs.T @ (weights[:, None] * derivs), weights


def constants():
    stiff, w = node_tables()
    mass = np.diag(w)
    kron = lambda a, b, c: np.kron(np.kron(a, b), c)
    volume = np.zeros((CUBE, CUBE))
    volume[:125, :125] = kron(stiff, mass, mass) + kron(mass, stiff, mass) + kron(mass, mass, stiff)
    high = volume.astype(jnp.bfloat16)
    low = (volume - high.astype(np.float64)).astype(jnp.bfloat16)
    volume = np.concatenate([high, high, low], axis=1)
    nodes = np.arange(125).reshape(5, 5, 5)
    layers = [nodes[0], nodes[4], nodes[:, 0], nodes[:, 4], nodes[:, :, 0], nodes[:, :, 4]]
    select = np.zeros((6 * ROWS, CUBE))
    for face, layer in enumerate(layers):
        select[face * ROWS + np.arange(WIDTH), layer.reshape(-1)] = 1.0
    lift = np.concatenate([select.T, select.T], axis=1)
    turn = np.zeros((8, ROWS, ROWS))
    for code in range(8):
        order = np.arange(WIDTH).reshape(5, 5)
        order = order[::-1] if code & 1 else order
        order = order[:, ::-1] if code & 2 else order
        order = order.T if code & 4 else order
        turn[code, np.arange(WIDTH), order.reshape(-1)] = 1.0
    back = np.swapaxes(turn, 1, 2)
    turns = [np.concatenate([m, m], axis=2).reshape(8 * ROWS, 2 * ROWS) for m in (turn, back)]
    face_mass = np.zeros((ROWS, 128))
    face_mass[:WIDTH] = np.outer(w, w).reshape(-1, 1)
    cube_mass = np.zeros((CUBE, 128))
    cube_mass[:125] = MASS * np.einsum("a,b,c->abc", w, w, w).reshape(-1, 1)
    bf = lambda a: jnp.asarray(np.asarray(a, np.float32), BF16)
    return (
        bf(volume),
        bf(select),
        bf(lift),
        bf(turns[0]),
        bf(turns[1]),
        jnp.asarray(np.concatenate([face_mass, cube_mass]), F32),
    )


def split(x):
    high = x.astype(BF16)
    return high, (x - high.astype(F32)).astype(BF16)


def dot(a, b):
    return jnp.dot(a, b, preferred_element_type=F32)


def dot_nt(a, b):
    return lax.dot_general(a, b, (((1,), (1,)), ((), ())), preferred_element_type=F32)


def ring_levels(total):
    levels, stride = [], 1
    while stride < total:
        rest = total // stride
        size = max(g for g in range(1, 33) if rest % g == 0)
        size = rest if size == 1 else size
        levels.append((stride, size))
        stride *= size
    return levels


def kernel(
    dims,
    rhs_ref, level_ref, own_ref, near_ref, kind_ref, orient_ref, pen_ref, send_ref, maps_ref,
    vol_ref, sel_ref, lift_ref, turn_ref, back_ref, mass_ref,
    x_out, r_out,
    field, gather, mapz, diag, psrc, pbuf, xsrc, xbuf, asrc, *rest,
):
    n_sfc, n_grp, count, ghost, pad = dims
    total = n_sfc * n_grp
    levels = ring_levels(total)
    slots_refs = rest[: len(levels)]
    psend, precv, xsend, xrecv, asend, arecv = rest[len(levels):]
    me = lax.axis_index("sfc") * n_grp + lax.axis_index("grp")
    slots = 6 * count
    entries = 4 * ghost
    cols = 4 * pad

    def place(device):
        return (device // n_grp, lax.rem(device, n_grp))

    def near_device(k):
        return place(lax.rem(me + OFFSETS[k] + total, total))

    def peer(level, step):
        stride, size = levels[level]
        digit = lax.rem(me // stride, size)
        return place(me + (lax.rem(digit + step, size) - digit) * stride)

    barrier = pltpu.get_barrier_semaphore()
    greeted = 0
    for level, (_, size) in enumerate(levels):
        def greet(step, carry, level=level):
            pl.semaphore_signal(barrier, inc=1, device_id=peer(level, step), device_id_type=MESH)
            return carry
        lax.fori_loop(1, size, greet, 0)
        greeted += size - 1
    if len(levels) > 1:
        for k in range(4):
            pl.semaphore_signal(barrier, inc=1, device_id=near_device(k), device_id_type=MESH)
        greeted += 4

    own = own_ref[...]
    high_slot = (own >> 8).astype(F32)
    low_slot = (own & 255).astype(F32)
    pen = pen_ref[...]
    pen_a = pen.astype(BF16).astype(F32)
    pen_b = (pen - pen_a).astype(BF16).astype(F32)
    pen_c = pen - pen_a - pen_b
    send = send_ref[...]
    zero_row = jnp.zeros_like(pen)
    params = jnp.concatenate(
        [high_slot, low_slot, kind_ref[...].astype(F32), orient_ref[...].astype(F32), pen_a, pen_b, pen_c, zero_row],
        axis=0,
    ).astype(BF16)
    sent_rows = jnp.concatenate(
        [(send >> 8).astype(F32), (send & 255).astype(F32)] + [zero_row] * 6, axis=0
    ).astype(BF16)
    near = jnp.broadcast_to(near_ref[...], (pad, entries))
    spot = lax.broadcasted_iota(jnp.int32, (pad, entries), 0)
    lane = lax.broadcasted_iota(jnp.int32, (pad, entries), 1)
    inside = spot < ghost
    order, spread = [], []
    for k in range(4):
        order.append(jnp.where(inside & (near == spot + (slots + k * ghost)), 1.0, 0.0).astype(BF16))
        spread.append(jnp.where(inside & (lane == spot + k * ghost), 1.0, 0.0).astype(BF16))
    ordered = dot_nt(params, jnp.concatenate(order, axis=0))
    spread = dot_nt(sent_rows, jnp.concatenate(spread, axis=0))
    own_slot = (ordered[0:1] * 256.0 + ordered[1:2]).astype(jnp.int32)
    send_slot = (spread[0:1] * 256.0 + spread[1:2]).astype(jnp.int32)
    slot_row = lax.broadcasted_iota(jnp.int32, (slots, cols), 0)
    gather[:, cols:] = jnp.where(slot_row == own_slot, 1.0, 0.0).astype(BF16)
    scale = jnp.exp2(-level_ref[...].astype(F32))
    scale_all = jnp.concatenate([jnp.broadcast_to(scale, (8, count))] * 6, axis=1).astype(BF16)
    own_scale = dot(scale_all, gather[:, cols:])[0:1]
    strength = (ordered[4:5] + ordered[5:6] + ordered[6:7]) * own_scale
    sub = lax.broadcasted_iota(jnp.int32, (8, cols), 0)
    tile = jnp.where(sub == 0, ordered[2:3], jnp.where(sub == 1, ordered[3:4], jnp.where(sub == 2, strength, 0.0)))
    for k in range(4):
        psrc[k] = tile[:, k * pad : (k + 1) * pad]

    pl.semaphore_wait(barrier, greeted)

    pcopies = []
    for k in range(4):
        pcopies.append(pltpu.make_async_remote_copy(
            src_ref=psrc.at[k], dst_ref=pbuf.at[k], send_sem=psend.at[k], recv_sem=precv.at[k],
            device_id=near_device(k ^ 1), device_id_type=MESH,
        ))
        pcopies[-1].start()

    gather[:, :cols] = jnp.where(slot_row == send_slot, 1.0, 0.0).astype(BF16)
    mapz[...] = jnp.zeros_like(mapz)
    for s in range(4):
        mapz[s * ROWS : s * ROWS + WIDTH, 0:WIDTH] = maps_ref[s]
    maps = mapz[...]
    map_high, map_low = split(maps[:, :ROWS])
    back_high, back_low = split(maps.T[:ROWS])
    back_twice = jnp.concatenate([back_high, back_high], axis=1)
    face_mass = jnp.concatenate([mass_ref[:ROWS]] * (cols // 128), axis=1)
    cube_mass = mass_ref[ROWS:]
    valid = [
        jnp.where((me + offset >= 0) & (me + offset < total), 1.0, 0.0).astype(F32) for offset in OFFSETS
    ]
    mass_scale = cube_mass * (scale * scale * scale)
    field[...] = jnp.zeros_like(field)
    for g in range(WIDTH):
        field[g * NODES : (g + 1) * NODES] = rhs_ref[g]
    right = field[...]

    def traces(v_high, v_low):
        both = dot(sel_ref[...], jnp.concatenate([v_high, v_low], axis=1))
        rows = [both[f * ROWS : (f + 1) * ROWS] for f in range(6)]
        return jnp.concatenate(
            [
                jnp.concatenate([row[:, :count] for row in rows], axis=1),
                jnp.concatenate([row[:, count:] for row in rows], axis=1),
            ],
            axis=0,
        ).astype(BF16)

    near_info = []
    xcopies = []

    def turned(values, codes, table):
        high, low = split(values)
        forms = dot(table[...], jnp.concatenate([high, low], axis=0))
        result = forms[:ROWS]
        for code in range(1, 8):
            result = jnp.where(codes == code, forms[code * ROWS : (code + 1) * ROWS], result)
        return result

    def operator(v, turn_number):
        v_high, v_low = split(v)
        picked = dot(traces(v_high, v_low), gather[...])
        picked = picked[:ROWS] + picked[ROWS:]
        own_side = picked[:, cols:]
        if not near_info:
            for copy in pcopies:
                copy.wait_recv()
            info = jnp.concatenate([pbuf[k] for k in range(4)], axis=1)
            near_info.append(info[0:1].astype(jnp.int32))
            near_info.append(info[1:2].astype(jnp.int32))
            power = jnp.concatenate([pbuf[k][2:3] * valid[k] for k in range(4)], axis=1)
            diag[:, :cols] = face_mass * power
            diag[:, cols:] = face_mass * strength
        kinds, codes = near_info
        oriented = turned(picked[:, :cols], codes, turn_ref)
        high, low = split(oriented)
        forms = dot(map_high, high) + dot(map_high, low) + dot(map_low, high)
        near_side = jnp.where(kinds == 1, oriented, 0.0)
        for s in range(4):
            near_side = jnp.where(kinds == s + 2, forms[s * ROWS : (s + 1) * ROWS], near_side)
        for k in range(4):
            xsrc[turn_number, k, :, :pad] = near_side[:, k * pad : (k + 1) * pad]
            xsrc[turn_number, k, :, pad:] = own_side[:, (k ^ 1) * pad : ((k ^ 1) + 1) * pad]
        copies = []
        for k in range(4):
            copies.append(pltpu.make_async_remote_copy(
                src_ref=xsrc.at[turn_number, k], dst_ref=xbuf.at[turn_number, k ^ 1],
                send_sem=xsend.at[turn_number, k], recv_sem=xrecv.at[turn_number, k ^ 1],
                device_id=near_device(k), device_id_type=MESH,
            ))
            copies[-1].start()
        xcopies.extend(copies)
        image = dot(vol_ref[:, : 2 * CUBE], jnp.concatenate([v_high, v_low], axis=0))
        image = (image + dot(vol_ref[:, 2 * CUBE :], v_high)) * scale + mass_scale * v
        for copy in copies:
            copy.wait_recv()
        near_got = jnp.concatenate([xbuf[turn_number, k, :, pad:] for k in range(4)], axis=1)
        own_got = jnp.concatenate([xbuf[turn_number, k ^ 1, :, :pad] * valid[k ^ 1] for k in range(4)], axis=1)
        near_flux = diag[:, :cols] * (near_side - near_got)
        own_flux = diag[:, cols:] * (own_side - own_got)
        stacked = jnp.concatenate([jnp.where(kinds == s + 2, near_flux, 0.0) for s in range(4)], axis=0)
        high, low = split(stacked)
        near_flux = jnp.where(kinds == 1, near_flux, 0.0)
        near_flux = near_flux + dot(back_twice, jnp.concatenate([high, low], axis=0)) + dot(back_low, high)
        near_flux = turned(near_flux, codes, back_ref)
        flux = jnp.concatenate([near_flux, own_flux], axis=1)
        faces = dot_nt(jnp.concatenate(split(flux), axis=0), gather[...])
        faces = faces[:ROWS] + faces[ROWS:]
        faces = jnp.concatenate([faces[:, f * count : (f + 1) * count] for f in range(6)], axis=0)
        return image + dot(lift_ref[...], jnp.concatenate(split(faces), axis=0))

    def level_copy(turn_number, level, step):
        return pltpu.make_async_remote_copy(
            src_ref=asrc.at[turn_number, level], dst_ref=slots_refs[level].at[turn_number, step - 1],
            send_sem=asend.at[turn_number, level], recv_sem=arecv.at[turn_number, level],
            device_id=peer(level, step), device_id_type=MESH,
        )

    def level_start(turn_number, level):
        def start(step, carry):
            level_copy(turn_number, level, step).start()
            return carry
        lax.fori_loop(1, levels[level][1], start, 0)

    def sums_start(turn_number, pairs):
        for i, (a, b) in enumerate(pairs):
            asrc[turn_number, 0, i : i + 1, :] = jnp.sum(a * b, axis=0, keepdims=True)
        level_start(turn_number, 0)

    def sums_wait(turn_number, number):
        for level in range(len(levels)):
            landed = slots_refs[level].at[turn_number]
            pltpu.make_async_copy(landed, landed, arecv.at[turn_number, level]).wait()
            value = asrc[turn_number, level] + jnp.sum(landed[...], axis=0)
            if level + 1 < len(levels):
                asrc[turn_number, level + 1] = value
                level_start(turn_number, level + 1)
        value = jnp.broadcast_to(jnp.sum(value, axis=1, keepdims=True), (8, 128))
        return [value[i : i + 1] for i in range(number)]

    asrc[...] = jnp.zeros_like(asrc)
    r = right
    w = operator(r, 0)
    x = p = s = z = None
    norm_last = None
    for it in range(ITERS):
        pairs = [(r, r), (r, w)]
        if it:
            pairs += [(r, s), (p, w), (p, s)]
        sums_start(it, pairs)
        q = operator(w, it + 1) if it + 1 < ITERS else None
        sums = sums_wait(it, len(pairs))
        norm = sums[0]
        if it == 0:
            alpha = norm / sums[1]
            p, s, z = r, w, q
            x = alpha * p
        else:
            beta = norm / norm_last
            alpha = norm / (sums[1] + beta * (sums[2] + sums[3]) + beta * beta * sums[4])
            p = r + beta * p
            s = w + beta * s
            x = x + alpha * p
            if q is not None:
                z = q + beta * z
        r = r - alpha * s
        if q is not None:
            w = w - alpha * z
        norm_last = norm

    field[...] = x
    for g in range(WIDTH):
        x_out[g] = field[g * NODES : (g + 1) * NODES]
    mapz[...] = r
    for g in range(WIDTH):
        r_out[g] = mapz[g * NODES : (g + 1) * NODES]

    for copy in pcopies + xcopies:
        copy.wait_send()
    for it in range(ITERS):
        for level in range(len(levels)):
            landed = slots_refs[level].at[it]
            pltpu.make_async_copy(landed, landed, asend.at[it, level]).wait()


def body(n_sfc, n_grp, right_side, cell_level, own_slot, near_slot, face_kind, orientation, penalty, send_slots, maps):
    count = right_side.shape[-1]
    ghost = send_slots.shape[0] // 4
    pad = -(-ghost // 128) * 128
    levels = ring_levels(n_sfc * n_grp)
    row = lambda a: a.reshape(1, -1)
    vmem = pl.BlockSpec(memory_space=pltpu.VMEM)
    dma = pltpu.SemaphoreType.DMA
    shape = jax.ShapeDtypeStruct((WIDTH, NODES, count), F32)
    x, r = pl.pallas_call(
        functools.partial(kernel, (n_sfc, n_grp, count, ghost, pad)),
        out_shape=(shape, shape),
        in_specs=[vmem] * 15,
        out_specs=(vmem, vmem),
        scratch_shapes=[
            pltpu.VMEM((CUBE, count), F32),
            pltpu.VMEM((6 * count, 8 * pad), BF16),
            pltpu.VMEM((4 * ROWS, 128), F32),
            pltpu.VMEM((ROWS, 8 * pad), F32),
            pltpu.VMEM((4, 8, pad), F32),
            pltpu.VMEM((4, 8, pad), F32),
            pltpu.VMEM((ITERS, 4, ROWS, 2 * pad), F32),
            pltpu.VMEM((ITERS, 4, ROWS, 2 * pad), F32),
            pltpu.VMEM((ITERS, len(levels), 8, 128), F32),
        ]
        + [pltpu.VMEM((ITERS, size - 1, 8, 128), F32) for _, size in levels]
        + [
            dma((4,)),
            dma((4,)),
            dma((ITERS, 4)),
            dma((ITERS, 4)),
            dma((ITERS, len(levels))),
            dma((ITERS, len(levels))),
        ],
        compiler_params=pltpu.CompilerParams(collective_id=0, has_side_effects=True),
    )(
        right_side.reshape(WIDTH, NODES, count),
        row(cell_level), row(own_slot), row(near_slot), row(face_kind), row(orientation), row(penalty), row(send_slots),
        maps, *constants(),
    )
    return x.reshape(right_side.shape), r.reshape(right_side.shape)


def solution(mesh):
    split_spec = P(("sfc", "grp"))
    field_spec = P(None, None, None, ("sfc", "grp"))
    return jax.shard_map(
        functools.partial(body, mesh.shape["sfc"], mesh.shape["grp"]),
        mesh=mesh,
        in_specs=(field_spec,) + (split_spec,) * 7 + (P(),),
        out_specs=(field_spec, field_spec),
        check_vma=False,
    )
```

time: 262 us -> 48.4 us (0.18)
  blocking collectives: 136 us -> 0 us
  starting transfers between devices: 40.1 us -> 0 us
  Pallas kernels: 0 us -> 39 us
  other arithmetic: 29.6 us -> 0 us
  local copies, waits for them, and re-layouts: 27.2 us -> 8.34 us
  waiting for transfers between devices: 11.6 us -> 0 us
  between operations: 11.9 us -> 0.66 us
  matrix products: 5.04 us -> 0 us
    psum x3 -> x0, blocking collectives: 136 us -> none  [body(): lax.psum((jnp.sum(residual * residual), jnp.sum(direction * image), jnp.s...]
    ppermute x18 -> x0, starting transfers between devices: 40.1 us -> none  [the longest x12 39.2 us: shifted(): return lax.ppermute(block, axis, route)]
    pallas_call x0 -> x1, Pallas kernels: none -> 39 us  [body(): pl.pallas_call(functools.partial(kernel, (n_sfc, n_grp, count, ghost, pad...]
    scatter-add x21 -> x0, other arithmetic: 22.9 us -> none  [the longest x3 8.54 us: apply_operator(): gathered = gathered.at[:, near_slot].add(near_term.reshape(width, -1))]
    gather x10 -> x0, local copies, waits for them, and re-layouts: 12.8 us -> none  [the longest x3 3.37 us: apply_operator(): own_values = jnp.take(pool, own_slot, axis=1).reshape(NODES, NODES, -1)]
    ppermute x18 -> x0, waiting for transfers between devices: 11.6 us -> none  [the longest x12 7.65 us: shifted(): return lax.ppermute(block, axis, route)]
    dot_general x15 -> x0, matrix products: 5.04 us -> none  [the longest x6 2.27 us: map_traces(): jnp.dot(stacked.reshape(4 * width, width), flat, precision=highest)]
    reduce_sum x10 -> x0, other arithmetic: 2.79 us -> none  [the longest x2 1.25 us: body(): jnp.sum(residual * residual)]
  transfers between devices with their start and end apart: 18 -> 0, of which waited for: 11 -> 0; matrix products, arithmetic and copies ran while one was open for 3% -> 0% of each run, Pallas kernels for 0% -> 0%
where the time goes in v1:
time: 48.4 us; the launch traced here: 48 us
  Pallas kernels  39 us (81%)
  local copies, waits for them, and re-layouts  8.34 us (17%)
  between operations  0.66 us (1%)
    pallas_call x1, Pallas kernels, body(): pl.pallas_call(functools.partial(kernel, (n_sfc, n_grp, count, ghost, pad...  39 us
    unnamed x17, local copies, waits for them, and re-layouts  4.94 us
    reshape x6, local copies, waits for them, and re-layouts, body(): row = lambda a: a.reshape(1, -1)  3.4 us

profile of v1, /device:TPU:0, one launch (start us, length us, event | category | flops | bytes accessed | tf_op | source)
XLA Modules:
  0.0 48.0 jit_solution(15742623335771966756)
XLA Ops:
  0.6 0.0 copy-start.1
  0.6 0.7 %copy-done.1 = s32[384]{0:T(512)S(1)} copy-done((s32[384]{0:T(512)S(1)}, s32[384]{0:T(512)}, u32[]{:S(2)}) %copy-start.1) | copy-done | bytes 1560
  1.3 0.0 copy-start.2
  1.3 0.6 %reshape.36.own_ref = s32[1,384]{1,0:T(1,128)} reshape(s32[384]{0:T(512)S(1)} %copy-done.1) | data formatting | bytes 3072 | tf_op jit(solution)/shard_map/reshape | solution.py:360
  1.9 0.1 copy-done.2
  2.0 0.0 copy-start.3
  2.0 0.6 %reshape.37.near_ref = s32[1,384]{1,0:T(1,128)} reshape(s32[384]{0:T(512)S(1)} %copy-done.2) | data formatting | bytes 3072 | tf_op jit(solution)/shard_map/reshape | solution.py:360
  2.6 0.1 copy-done.3
  2.7 0.0 copy-start.4
  2.7 0.5 %reshape.38.kind_ref = s32[1,384]{1,0:T(1,128)} reshape(s32[384]{0:T(512)S(1)} %copy-done.3) | data formatting | bytes 3072 | tf_op jit(solution)/shard_map/reshape | solution.py:360
  3.2 0.1 copy-done.4
  3.4 0.0 copy-start.5
  3.4 0.6 %reshape.39.orient_ref = s32[1,384]{1,0:T(1,128)} reshape(s32[384]{0:T(512)S(1)} %copy-done.4) | data formatting | bytes 3072 | tf_op jit(solution)/shard_map/reshape | solution.py:360
  3.9 0.1 copy-done.5
  4.0 0.0 copy-start.6
  4.0 0.6 %reshape.40.pen_ref = f32[1,384]{1,0:T(1,128)} reshape(f32[384]{0:T(512)S(1)} %copy-done.5) | data formatting | bytes 3072 | tf_op jit(solution)/shard_map/reshape | solution.py:360
  4.6 0.1 copy-done.6
  4.7 0.6 %reshape.41.send_ref = s32[1,384]{1,0:T(1,128)} reshape(s32[384]{0:T(512)S(1)} %copy-done.6) | data formatting | bytes 3072 | tf_op jit(solution)/shard_map/reshape | solution.py:360
  5.3 1.4 %copy.17.maps_ref = f32[4,25,25]{2,1,0:T(8,128)} copy(f32[4,25,25]{2,0,1:T(4,128)} %param.23) | data formatting | bytes 20000 | tf_op args[8]
  6.8 39.0 %shard_map.158 = (f32[25,5,128]{2,1,0:T(8,128)}, f32[25,5,128]{2,1,0:T(8,128)}) custom-call(f32[25,5,128]{2,1,0:T(8,128)} %bitcast.6, s32[1,128]{1,0:T(1,128)} %bitcast.7, s32[1,384]{1,0:T(1,128)} %reshape.36.own_ref, s32[1,384]{1,0:T(1,128)} %reshape.37.near_ref, s32[1,384]{1,0:T(1,128)} %reshape.38.kind_ref, s32[1,384]{1,0:T(1,128)} %reshape.39.orient_ref, ...), custom_call_target="tpu_custom_call" | custom-call | tf_op jit(solution)/shard_map/pallas_call | solution.py:364
  45.8 0.0 copy-start
  45.8 1.6 %copy.20 = f32[5,5,5,128]{3,2,1,0:T(8,128)} copy(f32[5,5,5,128]{3,2,1,0:T(8,128)} %bitcast.5) | data formatting | bytes 128000
  47.4 0.0 copy-done
  47.4 0.6 %copy.21 = f32[5,5,5,128]{3,2,1,0:T(8,128)} copy(f32[5,5,5,128]{3,2,1,0:T(8,128)S(1)} %bitcast.4) | data formatting | bytes 128000
Async XLA Ops:
  0.6 0.7 %copy-start.1 = (s32[384]{0:T(512)S(1)}, s32[384]{0:T(512)}, u32[]{:S(2)}) copy-start(s32[384]{0:T(512)} %param.17) | copy-start | bytes 4612
  1.3 0.7 %copy-start.2 = (s32[384]{0:T(512)S(1)}, s32[384]{0:T(512)}, u32[]{:S(2)}) copy-start(s32[384]{0:T(512)} %param.18) | copy-start | bytes 4612
  2.0 0.7 %copy-start.3 = (s32[384]{0:T(512)S(1)}, s32[384]{0:T(512)}, u32[]{:S(2)}) copy-start(s32[384]{0:T(512)} %param.19) | copy-start | bytes 4612
  2.7 0.7 %copy-start.4 = (s32[384]{0:T(512)S(1)}, s32[384]{0:T(512)}, u32[]{:S(2)}) copy-start(s32[384]{0:T(512)} %param.20) | copy-start | bytes 4612
  3.4 0.7 %copy-start.5 = (f32[384]{0:T(512)S(1)}, f32[384]{0:T(512)}, u32[]{:S(2)}) copy-start(f32[384]{0:T(512)} %param.21) | copy-start | bytes 4612
  4.0 0.7 %copy-start.6 = (s32[384]{0:T(512)S(1)}, s32[384]{0:T(512)}, u32[]{:S(2)}) copy-start(s32[384]{0:T(512)} %param.22) | copy-start | bytes 4612
  45.8 1.6 %copy-start = (f32[25,5,128]{2,1,0:T(8,128)S(1)}, f32[25,5,128]{2,1,0:T(8,128)}, u32[]{:S(2)}) copy-start(f32[25,5,128]{2,1,0:T(8,128)} %get-tuple-element.5) | copy-start | bytes 192004

commit v2 on v1

--- a/solution.py
+++ b/solution.py
@@ -123,6 +123,20 @@
         digit = lax.rem(me // stride, size)
         return place(me + (lax.rem(digit + step, size) - digit) * stride)
 
+    exists = [(me + offset >= 0) & (me + offset < total) for offset in OFFSETS]
+
+    def guarded(k, action):
+        @pl.when(exists[k])
+        def _():
+            action()
+
+    for k in range(4):
+        @pl.when(jnp.logical_not(exists[k]))
+        def _(k=k):
+            pbuf[k] = jnp.zeros((8, pad), F32)
+            for it in range(ITERS):
+                xbuf[it, k] = jnp.zeros((ROWS, 2 * pad), F32)
+
     barrier = pltpu.get_barrier_semaphore()
     greeted = 0
     for level, (_, size) in enumerate(levels):
@@ -136,23 +150,24 @@
             pl.semaphore_signal(barrier, inc=1, device_id=near_device(k), device_id_type=MESH)
         greeted += 4
 
-    own = own_ref[...]
+    line = lambda ref: ref[...].reshape(1, -1)
+    own = line(own_ref)
     high_slot = (own >> 8).astype(F32)
     low_slot = (own & 255).astype(F32)
-    pen = pen_ref[...]
+    pen = line(pen_ref)
     pen_a = pen.astype(BF16).astype(F32)
     pen_b = (pen - pen_a).astype(BF16).astype(F32)
     pen_c = pen - pen_a - pen_b
-    send = send_ref[...]
+    send = line(send_ref)
     zero_row = jnp.zeros_like(pen)
     params = jnp.concatenate(
-        [high_slot, low_slot, kind_ref[...].astype(F32), orient_ref[...].astype(F32), pen_a, pen_b, pen_c, zero_row],
+        [high_slot, low_slot, line(kind_ref).astype(F32), line(orient_ref).astype(F32), pen_a, pen_b, pen_c, zero_row],
         axis=0,
     ).astype(BF16)
     sent_rows = jnp.concatenate(
         [(send >> 8).astype(F32), (send & 255).astype(F32)] + [zero_row] * 6, axis=0
     ).astype(BF16)
-    near = jnp.broadcast_to(near_ref[...], (pad, entries))
+    near = jnp.broadcast_to(line(near_ref), (pad, entries))
     spot = lax.broadcasted_iota(jnp.int32, (pad, entries), 0)
     lane = lax.broadcasted_iota(jnp.int32, (pad, entries), 1)
     inside = spot < ghost
@@ -166,7 +181,7 @@
     send_slot = (spread[0:1] * 256.0 + spread[1:2]).astype(jnp.int32)
     slot_row = lax.broadcasted_iota(jnp.int32, (slots, cols), 0)
     gather[:, cols:] = jnp.where(slot_row == own_slot, 1.0, 0.0).astype(BF16)
-    scale = jnp.exp2(-level_ref[...].astype(F32))
+    scale = jnp.exp2(-line(level_ref).astype(F32))
     scale_all = jnp.concatenate([jnp.broadcast_to(scale, (8, count))] * 6, axis=1).astype(BF16)
     own_scale = dot(scale_all, gather[:, cols:])[0:1]
     strength = (ordered[4:5] + ordered[5:6] + ordered[6:7]) * own_scale
@@ -183,21 +198,18 @@
             src_ref=psrc.at[k], dst_ref=pbuf.at[k], send_sem=psend.at[k], recv_sem=precv.at[k],
             device_id=near_device(k ^ 1), device_id_type=MESH,
         ))
-        pcopies[-1].start()
+        guarded(k ^ 1, pcopies[-1].start)
 
     gather[:, :cols] = jnp.where(slot_row == send_slot, 1.0, 0.0).astype(BF16)
     mapz[...] = jnp.zeros_like(mapz)
     for s in range(4):
-        mapz[s * ROWS : s * ROWS + WIDTH, 0:WIDTH] = maps_ref[s]
+        mapz[s * ROWS : s * ROWS + WIDTH, 0:WIDTH] = maps_ref[:, s, :]
     maps = mapz[...]
     map_high, map_low = split(maps[:, :ROWS])
     back_high, back_low = split(maps.T[:ROWS])
     back_twice = jnp.concatenate([back_high, back_high], axis=1)
     face_mass = jnp.concatenate([mass_ref[:ROWS]] * (cols // 128), axis=1)
     cube_mass = mass_ref[ROWS:]
-    valid = [
-        jnp.where((me + offset >= 0) & (me + offset < total), 1.0, 0.0).astype(F32) for offset in OFFSETS
-    ]
     mass_scale = cube_mass * (scale * scale * scale)
     field[...] = jnp.zeros_like(field)
     for g in range(WIDTH):
@@ -232,12 +244,12 @@
         picked = picked[:ROWS] + picked[ROWS:]
         own_side = picked[:, cols:]
         if not near_info:
-            for copy in pcopies:
-                copy.wait_recv()
+            for k in range(4):
+                guarded(k, pcopies[k].wait_recv)
             info = jnp.concatenate([pbuf[k] for k in range(4)], axis=1)
             near_info.append(info[0:1].astype(jnp.int32))
             near_info.append(info[1:2].astype(jnp.int32))
-            power = jnp.concatenate([pbuf[k][2:3] * valid[k] for k in range(4)], axis=1)
+            power = jnp.concatenate([pbuf[k][2:3] for k in range(4)], axis=1)
             diag[:, :cols] = face_mass * power
             diag[:, cols:] = face_mass * strength
         kinds, codes = near_info
@@ -257,14 +269,14 @@
                 send_sem=xsend.at[turn_number, k], recv_sem=xrecv.at[turn_number, k ^ 1],
                 device_id=near_device(k), device_id_type=MESH,
             ))
-            copies[-1].start()
-        xcopies.extend(copies)
+            guarded(k, copies[-1].start)
+        xcopies.append(copies)
         image = dot(vol_ref[:, : 2 * CUBE], jnp.concatenate([v_high, v_low], axis=0))
         image = (image + dot(vol_ref[:, 2 * CUBE :], v_high)) * scale + mass_scale * v
-        for copy in copies:
-            copy.wait_recv()
+        for k in range(4):
+            guarded(k ^ 1, copies[k].wait_recv)
         near_got = jnp.concatenate([xbuf[turn_number, k, :, pad:] for k in range(4)], axis=1)
-        own_got = jnp.concatenate([xbuf[turn_number, k ^ 1, :, :pad] * valid[k ^ 1] for k in range(4)], axis=1)
+        own_got = jnp.concatenate([xbuf[turn_number, k ^ 1, :, :pad] for k in range(4)], axis=1)
         near_flux = diag[:, :cols] * (near_side - near_got)
         own_flux = diag[:, cols:] * (own_side - own_got)
         stacked = jnp.concatenate([jnp.where(kinds == s + 2, near_flux, 0.0) for s in range(4)], axis=0)
@@ -344,8 +356,10 @@
     for g in range(WIDTH):
         r_out[g] = mapz[g * NODES : (g + 1) * NODES]
 
-    for copy in pcopies + xcopies:
-        copy.wait_send()
+    for k in range(4):
+        guarded(k ^ 1, pcopies[k].wait_send)
+        for copies in xcopies:
+            guarded(k, copies[k].wait_send)
     for it in range(ITERS):
         for level in range(len(levels)):
             landed = slots_refs[level].at[it]
@@ -357,7 +371,6 @@
     ghost = send_slots.shape[0] // 4
     pad = -(-ghost // 128) * 128
     levels = ring_levels(n_sfc * n_grp)
-    row = lambda a: a.reshape(1, -1)
     vmem = pl.BlockSpec(memory_space=pltpu.VMEM)
     dma = pltpu.SemaphoreType.DMA
     shape = jax.ShapeDtypeStruct((WIDTH, NODES, count), F32)
@@ -389,8 +402,8 @@
         compiler_params=pltpu.CompilerParams(collective_id=0, has_side_effects=True),
     )(
         right_side.reshape(WIDTH, NODES, count),
-        row(cell_level), row(own_slot), row(near_slot), row(face_kind), row(orientation), row(penalty), row(send_slots),
-        maps, *constants(),
+        cell_level, own_slot, near_slot, face_kind, orientation, penalty, send_slots,
+        jnp.swapaxes(maps, 0, 1), *constants(),
     )
     return x.reshape(right_side.shape), r.reshape(right_side.shape)
 

time: 48.4 us -> 39.9 us (0.82)
  local copies, waits for them, and re-layouts: 8.34 us -> 2.22 us
  Pallas kernels: 39 us -> 36.8 us
    reshape x6 -> x0, local copies, waits for them, and re-layouts: 3.4 us -> none  [body(): row = lambda a: a.reshape(1, -1)]
    unnamed x17 -> x4, local copies, waits for them, and re-layouts: 4.94 us -> 2.22 us
    pallas_call x1, Pallas kernels: 39 us -> 36.8 us  [body(): pl.pallas_call(functools.partial(kernel, (n_sfc, n_grp, count, ghost, pad...]
where the time goes in v2:
time: 39.9 us; the launch traced here: 39.7 us
  Pallas kernels  36.8 us (92%)
  local copies, waits for them, and re-layouts  2.22 us (6%)
  between operations  0.65 us (2%)
    pallas_call x1, Pallas kernels, body(): pl.pallas_call(functools.partial(kernel, (n_sfc, n_grp, count, ghost, pad...  36.8 us
    unnamed x4, local copies, waits for them, and re-layouts  2.22 us

profile of v2, /device:TPU:0, one launch (start us, length us, event | category | flops | bytes accessed | tf_op | source)
XLA Modules:
  0.0 39.7 jit_solution(18037402475729472617)
XLA Ops:
  0.6 36.8 %shard_map.158 = (f32[25,5,128]{2,1,0:T(8,128)}, f32[25,5,128]{2,1,0:T(8,128)}) custom-call(f32[25,5,128]{2,1,0:T(8,128)} %bitcast.6, s32[128]{0:T(128)} %level_ref.1, s32[384]{0:T(512)} %own_ref.1, s32[384]{0:T(512)} %near_ref.1, s32[384]{0:T(512)} %kind_ref.1, s32[384]{0:T(512)} %orient_ref.1, f32[384]{0:T(512)} %pen_ref.1, s32[384]{0:T(512)} %send_ref.1, ...), custom_call_target="tpu_custom_call" | custom-call | tf_op jit(solution)/shard_map/pallas_call | solution.py:377
  37.5 0.0 copy-start
  37.5 1.6 %copy.19 = f32[5,5,5,128]{3,2,1,0:T(8,128)} copy(f32[5,5,5,128]{3,2,1,0:T(8,128)} %bitcast.5) | data formatting | bytes 128000
  39.1 0.0 copy-done
  39.1 0.6 %copy.20 = f32[5,5,5,128]{3,2,1,0:T(8,128)} copy(f32[5,5,5,128]{3,2,1,0:T(8,128)S(1)} %bitcast.4) | data formatting | bytes 128000
Async XLA Ops:
  37.5 1.6 %copy-start = (f32[25,5,128]{2,1,0:T(8,128)S(1)}, f32[25,5,128]{2,1,0:T(8,128)}, u32[]{:S(2)}) copy-start(f32[25,5,128]{2,1,0:T(8,128)} %get-tuple-element.5) | copy-start | bytes 192004

commit v3 on v2

--- a/solution.py
+++ b/solution.py
@@ -95,6 +95,28 @@
     return levels
 
 
+def tail_rows(ghost, pad):
+    return ROWS // 2 if pad == 128 and 64 < ghost <= 96 else ROWS
+
+
+def pack(first, second, ghost, pad):
+    if tail_rows(ghost, pad) == ROWS:
+        return first, second
+    lane = lax.broadcasted_iota(jnp.int32, (ROWS, pad), 1)
+    half = ROWS // 2
+    moved = pltpu.roll(second, ghost, 1)
+    tail = jnp.where(lane[:half] < 64, moved[:half], pltpu.roll(moved[half:], 64, 1))
+    return jnp.where(lane < ghost, first, moved), tail
+
+
+def unpack(main, tail, ghost, pad):
+    if tail_rows(ghost, pad) == ROWS:
+        return main, tail
+    lane = lax.broadcasted_iota(jnp.int32, (ROWS, pad), 1)
+    moved = jnp.concatenate([tail, pltpu.roll(tail, 64, 1)], axis=0)
+    return main, pltpu.roll(jnp.where(lane < ghost, moved, main), pad - ghost, 1)
+
+
 def kernel(
     dims,
     rhs_ref, level_ref, own_ref, near_ref, kind_ref, orient_ref, pen_ref, send_ref, maps_ref,
@@ -135,7 +157,7 @@
         def _(k=k):
             pbuf[k] = jnp.zeros((8, pad), F32)
             for it in range(ITERS):
-                xbuf[it, k] = jnp.zeros((ROWS, 2 * pad), F32)
+                xbuf[it, k] = jnp.zeros(xbuf.shape[2:], F32)
 
     barrier = pltpu.get_barrier_semaphore()
     greeted = 0
@@ -260,8 +282,11 @@
         for s in range(4):
             near_side = jnp.where(kinds == s + 2, forms[s * ROWS : (s + 1) * ROWS], near_side)
         for k in range(4):
-            xsrc[turn_number, k, :, :pad] = near_side[:, k * pad : (k + 1) * pad]
-            xsrc[turn_number, k, :, pad:] = own_side[:, (k ^ 1) * pad : ((k ^ 1) + 1) * pad]
+            main, tail = pack(
+                near_side[:, k * pad : (k + 1) * pad], own_side[:, (k ^ 1) * pad : ((k ^ 1) + 1) * pad], ghost, pad
+            )
+            xsrc[turn_number, k, :ROWS] = main
+            xsrc[turn_number, k, ROWS:] = tail
         copies = []
         for k in range(4):
             copies.append(pltpu.make_async_remote_copy(
@@ -269,14 +294,16 @@
                 send_sem=xsend.at[turn_number, k], recv_sem=xrecv.at[turn_number, k ^ 1],
                 device_id=near_device(k), device_id_type=MESH,
             ))
-            guarded(k, copies[-1].start)
+        for k in (2, 3, 0, 1):
+            guarded(k, copies[k].start)
         xcopies.append(copies)
         image = dot(vol_ref[:, : 2 * CUBE], jnp.concatenate([v_high, v_low], axis=0))
         image = (image + dot(vol_ref[:, 2 * CUBE :], v_high)) * scale + mass_scale * v
         for k in range(4):
             guarded(k ^ 1, copies[k].wait_recv)
-        near_got = jnp.concatenate([xbuf[turn_number, k, :, pad:] for k in range(4)], axis=1)
-        own_got = jnp.concatenate([xbuf[turn_number, k ^ 1, :, :pad] for k in range(4)], axis=1)
+        got = [unpack(xbuf[turn_number, k, :ROWS], xbuf[turn_number, k, ROWS:], ghost, pad) for k in range(4)]
+        near_got = jnp.concatenate([got[k][1] for k in range(4)], axis=1)
+        own_got = jnp.concatenate([got[k ^ 1][0] for k in range(4)], axis=1)
         near_flux = diag[:, :cols] * (near_side - near_got)
         own_flux = diag[:, cols:] * (own_side - own_got)
         stacked = jnp.concatenate([jnp.where(kinds == s + 2, near_flux, 0.0) for s in range(4)], axis=0)
@@ -304,8 +331,12 @@
         lax.fori_loop(1, levels[level][1], start, 0)
 
     def sums_start(turn_number, pairs):
+        lane = lax.broadcasted_iota(jnp.int32, (1, 128), 1)
+        row = jnp.zeros((1, 128), F32)
         for i, (a, b) in enumerate(pairs):
-            asrc[turn_number, 0, i : i + 1, :] = jnp.sum(a * b, axis=0, keepdims=True)
+            part = jnp.sum(jnp.sum(a * b, axis=0, keepdims=True), axis=1, keepdims=True)
+            row = jnp.where(lane == i, part, row)
+        asrc[turn_number, 0] = row
         level_start(turn_number, 0)
 
     def sums_wait(turn_number, number):
@@ -316,8 +347,7 @@
             if level + 1 < len(levels):
                 asrc[turn_number, level + 1] = value
                 level_start(turn_number, level + 1)
-        value = jnp.broadcast_to(jnp.sum(value, axis=1, keepdims=True), (8, 128))
-        return [value[i : i + 1] for i in range(number)]
+        return [value[:, i : i + 1] for i in range(number)]
 
     asrc[...] = jnp.zeros_like(asrc)
     r = right
@@ -386,11 +416,11 @@
             pltpu.VMEM((ROWS, 8 * pad), F32),
             pltpu.VMEM((4, 8, pad), F32),
             pltpu.VMEM((4, 8, pad), F32),
-            pltpu.VMEM((ITERS, 4, ROWS, 2 * pad), F32),
-            pltpu.VMEM((ITERS, 4, ROWS, 2 * pad), F32),
-            pltpu.VMEM((ITERS, len(levels), 8, 128), F32),
+            pltpu.VMEM((ITERS, 4, ROWS + tail_rows(ghost, pad), pad), F32),
+            pltpu.VMEM((ITERS, 4, ROWS + tail_rows(ghost, pad), pad), F32),
+            pltpu.VMEM((ITERS, len(levels), 1, 128), F32),
         ]
-        + [pltpu.VMEM((ITERS, size - 1, 8, 128), F32) for _, size in levels]
+        + [pltpu.VMEM((ITERS, size - 1, 1, 128), F32) for _, size in levels]
         + [
             dma((4,)),
             dma((4,)),

time: 39.9 us -> 38.6 us (0.967)
  Pallas kernels: 36.8 us -> 35.5 us
    pallas_call x1, Pallas kernels: 36.8 us -> 35.5 us  [body(): pl.pallas_call(functools.partial(kernel, (n_sfc, n_grp, count, ghost, pad...]
where the time goes in v3:
time: 38.6 us; the launch traced here: 38.4 us
  Pallas kernels  35.5 us (92%)
  local copies, waits for them, and re-layouts  2.22 us (6%)
  between operations  0.65 us (2%)
    pallas_call x1, Pallas kernels, body(): pl.pallas_call(functools.partial(kernel, (n_sfc, n_grp, count, ghost, pad...  35.5 us
    unnamed x4, local copies, waits for them, and re-layouts  2.22 us

profile of v3, /device:TPU:0, one launch (start us, length us, event | category | flops | bytes accessed | tf_op | source)
XLA Modules:
  0.0 38.4 jit_solution(4424516908528499568)
XLA Ops:
  0.6 35.5 %shard_map.158 = (f32[25,5,128]{2,1,0:T(8,128)}, f32[25,5,128]{2,1,0:T(8,128)}) custom-call(f32[25,5,128]{2,1,0:T(8,128)} %bitcast.6, s32[128]{0:T(128)} %level_ref.1, s32[384]{0:T(512)} %own_ref.1, s32[384]{0:T(512)} %near_ref.1, s32[384]{0:T(512)} %kind_ref.1, s32[384]{0:T(512)} %orient_ref.1, f32[384]{0:T(512)} %pen_ref.1, s32[384]{0:T(512)} %send_ref.1, ...), custom_call_target="tpu_custom_call" | custom-call | tf_op jit(solution)/shard_map/pallas_call | solution.py:407
  36.1 0.0 copy-start
  36.2 1.6 %copy.19 = f32[5,5,5,128]{3,2,1,0:T(8,128)} copy(f32[5,5,5,128]{3,2,1,0:T(8,128)} %bitcast.5) | data formatting | bytes 128000
  37.7 0.0 copy-done
  37.7 0.6 %copy.20 = f32[5,5,5,128]{3,2,1,0:T(8,128)} copy(f32[5,5,5,128]{3,2,1,0:T(8,128)S(1)} %bitcast.4) | data formatting | bytes 128000
Async XLA Ops:
  36.1 1.6 %copy-start = (f32[25,5,128]{2,1,0:T(8,128)S(1)}, f32[25,5,128]{2,1,0:T(8,128)}, u32[]{:S(2)}) copy-start(f32[25,5,128]{2,1,0:T(8,128)} %get-tuple-element.5) | copy-start | bytes 192004
